TPU v7x, 32 devices: a whole 2x2x4 slice. The times are simulated.
32 devices in a mesh: gx: 8 (over z, y), gy: 4 (over x, core).
Axes of the slice: x: 2, y: 2, z: 4, core: 2. Of those that a mesh axis runs over, the one named last changes fastest.
Arguments:
- coarse_send: bfloat16 [8, 35, 4096], P('gx', None, 'gy'), may hold values from -6 to 6
- coarse_flux: float32 [8, 35, 1024], P('gx', None, 'gy'), may hold values from -6 to 6
- patch_owner: int32 [8], replicated, may hold values from 0 to 15, as said below
- velocity: float32 [3], replicated, may hold values from -0.6 to 0.6
- diffusivity: float32 [35], replicated, may hold values from 0.03 to 0.15
- stoich: float32 [35, 35], replicated, may hold values from -1 to 1
Outputs:
- fine_state: float32 [16, 35, 32768], P('gx', None, 'gy')
- reflux: float32 [8, 35, 1024], P('gx', None, 'gy')
Inputs may be any that keep to these rules, and one draw needn't show every extreme that they name: `patch_owner`: the 8 entries are distinct; slot s belongs to owner group s // 2, the group of index s // 2 along gx; a group owns 0, 1 or 2 patches, and at least one group owns exactly 2.
All inputs are finite; a program needn't handle non-finite values.
Results may differ from a plain program's by a relative error of at most 0.0003.
Values may be sent and summed in bfloat16 or wider, within the bound.
A program may use at most 128 MiB of HBM per device.

v0:
```python
import functools

import jax
import jax.numpy as jnp
import numpy as np
from jax import lax
from jax.experimental import pallas as pl
from jax.experimental.pallas import tpu as pltpu
from jax.sharding import PartitionSpec as P

time_step = 0.25
LANES = 128


def round_up(count, step):
    return -(-count // step) * step


def refine_matrix(edge):
    fine = 2 * edge
    copy_1d = np.zeros((edge, fine), np.float32)
    slope_1d = np.zeros((edge, fine), np.float32)
    for j in range(fine):
        i, sign = j // 2, (j % 2 - 0.5) * 0.5
        copy_1d[i, j] = 1.0
        low, high = max(i - 1, 0), min(i + 1, edge - 1)
        scale = sign * (0.5 if high - low == 2 else 1.0)
        slope_1d[high, j] += scale
        slope_1d[low, j] -= scale
    copies = np.einsum("ab,cd->acbd", copy_1d, copy_1d)
    shape = (edge * edge, fine * fine)
    planar = copies + np.einsum("ab,cd->acbd", copy_1d, slope_1d) + np.einsum("ab,cd->acbd", slope_1d, copy_1d)
    return np.concatenate([planar.reshape(shape), copies.reshape(shape)], 1)


def side_matrix(edge):
    fine = 2 * edge
    pick = np.zeros((fine, fine, 4, edge), np.float32)
    for along in range(fine):
        pick[along, 0, 0, along // 2] = 1.0
        pick[along, fine - 1, 1, along // 2] = 1.0
        pick[0, along, 2, along // 2] = 1.0
        pick[fine - 1, along, 3, along // 2] = 1.0
    pick = pick.reshape(fine * fine, 4 * edge)
    return np.tile(pick, (1, max(1, LANES // (4 * edge))))


def split_halves(values):
    high = values.astype(jnp.bfloat16)
    low = (values - high.astype(jnp.float32)).astype(jnp.bfloat16)
    return high, low


def react_layer(source, index, react):
    rows, width = source.shape[1:]
    field_rows = react.shape[1] // 3
    rate = 1.0 / (1.0 + jnp.exp(-2.0 * source[index, 0:1, :]))
    reacting = source[index] * rate
    reacting = jnp.concatenate([reacting, jnp.zeros((field_rows - rows, width), jnp.float32)], 0)
    high, low = split_halves(reacting)
    return jnp.dot(react[...], jnp.concatenate([high, high, low], 0), preferred_element_type=jnp.float32)


def run_layers(source, start, count, coefs, react, produced, fine, use):
    produced[...] = react_layer(source, start, react)

    @pl.loop(0, count)
    def _(layer):
        following = react_layer(source, start + layer + 1, react)
        use(layer, step_layer(source, start + layer, coefs, produced, fine))
        produced[...] = following


def step_layer(source, index, coefs, produced, fine):
    rows, width = source.shape[1:]
    tiles = width // LANES
    lane = lax.broadcasted_iota(jnp.int32, (8, LANES), 1)
    column = lax.rem(lane, fine)
    first_x, last_x = column == 0, column == fine - 1
    up_mask, down_mask = lane < LANES - fine, lane >= fine
    pieces = []
    for group in range(rows // 8):
        band = slice(8 * group, 8 * group + 8)
        cells = [source[index, band, LANES * t : LANES * (t + 1)] for t in range(tiles)]
        raised = [pltpu.roll(c, LANES - fine, 1) for c in cells]
        lowered = [pltpu.roll(c, fine, 1) for c in cells]
        across = []
        for t in range(tiles):
            span = slice(LANES * t, LANES * (t + 1))
            c = cells[t]
            x_high = jnp.where(last_x, c, pltpu.roll(c, LANES - 1, 1))
            x_low = jnp.where(first_x, c, pltpu.roll(c, 1, 1))
            y_high = jnp.where(up_mask, raised[t], raised[t + 1] if t + 1 < tiles else c)
            y_low = jnp.where(down_mask, lowered[t], lowered[t - 1] if t else c)
            z_high = source[index + 1, band, span]
            z_low = source[index - 1, band, span]
            total = coefs[0, band, :] * x_high + coefs[1, band, :] * x_low
            total += coefs[2, band, :] * y_high + coefs[3, band, :] * y_low
            total += coefs[4, band, :] * z_high + coefs[5, band, :] * z_low
            total += coefs[6, band, :] * c
            across.append(total + produced[band, span])
        pieces.append(across)
    return pieces


def store_layer(target, index, pieces):
    for group, across in enumerate(pieces):
        for t, value in enumerate(across):
            target[index, 8 * group : 8 * group + 8, LANES * t : LANES * (t + 1)] = value


def fill_layers(coarse, matrix, spread, state, at_bottom, at_top):
    held, padded_rows, cells = coarse.shape
    rows, width = state.shape[1:]
    flat = coarse[...].reshape(held * padded_rows, cells)
    spread[...] = jnp.dot(flat, matrix[...], preferred_element_type=jnp.float32)

    def copies(layer):
        return spread[pl.ds(layer * padded_rows, rows), width:]

    @pl.when(at_bottom)
    def _():
        spread[pl.ds(1 * padded_rows, rows), width:] = 2.0 * copies(2) - copies(3)

    @pl.when(at_top)
    def _():
        top = held - 2
        spread[pl.ds(top * padded_rows, rows), width:] = 2.0 * copies(top - 1) - copies(top - 2)

    for layer in range(1, held - 1):
        planar = spread[pl.ds(layer * padded_rows, rows), :width]
        slope = (copies(layer + 1) - copies(layer - 1)) * 0.125
        state[2 * layer - 2] = planar - slope
        state[2 * layer - 1] = planar + slope

    @pl.when(at_bottom)
    def _():
        state[1] = state[2]

    @pl.when(at_top)
    def _():
        state[2 * held - 6] = state[2 * held - 7]


def pencil_ends():
    pencil = lax.axis_index("gy")
    return pencil == 0, pencil == lax.axis_size("gy") - 1


def prepare(velocity, diffusivity, stoich, coefs, react, table):
    fields = stoich.shape[0]
    rows = coefs.shape[1]
    part = react.shape[1] // 3
    table[...] = jnp.zeros(table.shape, jnp.float32)
    table[:fields, :fields] = stoich[...] * time_step
    scaled = table[...]
    high = scaled.astype(jnp.bfloat16).astype(jnp.float32)
    low = scaled - high
    joined = high + pltpu.roll(low, part, 1) + pltpu.roll(high, 2 * part, 1)
    react[...] = joined[:, : 3 * part].astype(jnp.bfloat16)
    table[...] = jnp.zeros(table.shape, jnp.float32)
    table[0:1, :fields] = diffusivity[...]
    shape = (rows, LANES)
    diagonal = lax.broadcasted_iota(jnp.int32, shape, 0) == lax.broadcasted_iota(jnp.int32, shape, 1)
    line = jnp.broadcast_to(table[0:1, :LANES], shape)
    column = jnp.sum(jnp.where(diagonal, line, 0.0), 1, keepdims=True)
    diffuse = jnp.broadcast_to(column, shape)
    for dim in range(3):
        half_speed = velocity[dim] * 0.5
        coefs[2 * dim] = (diffuse - half_speed) * time_step
        coefs[2 * dim + 1] = (diffuse + half_speed) * time_step
    coefs[6] = 1.0 - 6.0 * time_step * diffuse


def prepared(fields):
    rows, padded_rows = round_up(fields, 8), round_up(fields, 16)
    return (
        jax.ShapeDtypeStruct((7, rows, LANES), jnp.float32),
        jax.ShapeDtypeStruct((rows, 3 * padded_rows), jnp.bfloat16),
    ), [pltpu.VMEM((rows, round_up(3 * padded_rows, LANES)), jnp.float32)]


def fine_kernel(
    fine, coarse_hbm, matrix_hbm, coefs_hbm, react_hbm, out, coarse, matrix, coefs, react, in_sems, produced, spread, state, middle, ready, sems,
):
    pairs = ((coarse_hbm, coarse), (matrix_hbm, matrix), (coefs_hbm, coefs), (react_hbm, react))
    fetches = [pltpu.make_async_copy(source, target, in_sems.at[i]) for i, (source, target) in enumerate(pairs)]
    for copy in fetches:
        copy.start()
    for copy in fetches[:2]:
        copy.wait()
    at_bottom, at_top = pencil_ends()
    slots = out.shape[2] * LANES // state.shape[2]
    fields = out.shape[0]
    layers = out.shape[1]
    step = out.shape[2]

    def copy_out(layer):
        return pltpu.make_async_copy(
            ready.at[layer],
            out.at[:, layer],
            sems.at[layer],
        )

    for slot in range(slots):
        fill_layers(coarse.at[slot], matrix, spread, state, at_bottom, at_top)
        if slot == 0:
            for copy in fetches[2:]:
                copy.wait()

        def to_middle(layer, pieces):
            store_layer(middle, layer, pieces)

        run_layers(state, 1, layers + 2, coefs, react, produced, fine, to_middle)

        @pl.when(at_bottom)
        def _():
            middle[0] = middle[1]

        @pl.when(at_top)
        def _():
            middle[layers + 1] = middle[layers]

        def to_output(layer, pieces):
            for group, across in enumerate(pieces):
                low, high = 8 * group, min(8 * group + 8, fields)
                for t, value in enumerate(across):
                    span = slice(LANES * t, LANES * (t + 1))
                    half = (value + state[layer + 2, low : low + 8, span]) * 0.5
                    lines = ready.at[layer].reshape(fields * step, LANES)
                    lines[pl.ds(low * step + t * slots + slot, high - low, stride=step), :] = half[: high - low]

            if slot == slots - 1:
                copy_out(layer).start()

        run_layers(middle, 1, layers, coefs, react, produced, fine, to_output)

    for layer in range(layers):
        copy_out(layer).wait()


def side_sums(fine, coarse, matrix, coefs, react, sides, velocity, flux, out, produced, spread, state, sums):
    at_bottom, at_top = pencil_ends()
    fields = out.shape[0]
    rows, width = state.shape[1:]
    layers = state.shape[0] - 4
    fill_layers(coarse, matrix, spread, state, at_bottom, at_top)

    def to_sums(layer, pieces):
        for group, across in enumerate(pieces):
            band = slice(8 * group, 8 * group + 8)
            for t, value in enumerate(across):
                span = slice(LANES * t, LANES * (t + 1))
                sums[layer, band, span] = value + state[layer + 2, band, span]

    run_layers(state, 2, layers, coefs, react, produced, fine, to_sums)
    pads = jnp.zeros((round_up(rows, 16) - rows, width), jnp.float32)
    halves = []
    for pair in range(layers // 2):
        high, low = split_halves(jnp.concatenate([sums[2 * pair] + sums[2 * pair + 1], pads], 0))
        halves += [high, low]
    picked = jnp.dot(jnp.concatenate(halves, 0), sides[...], preferred_element_type=jnp.float32)
    step = rows + pads.shape[0]
    each = [
        picked[2 * step * i : 2 * step * i + rows] + picked[2 * step * i + step : 2 * step * i + step + rows]
        for i in range(layers // 2)
    ]
    span = sides.shape[1]
    per_tile = span // (fine * 2)
    lane = lax.broadcasted_iota(jnp.int32, (rows, span), 1)
    for tile in range(len(each) // per_tile):
        value = each[tile * per_tile]
        for i in range(1, per_tile):
            value = jnp.where(lane >= i * fine * 2, each[tile * per_tile + i], value)
        along_x = lax.rem(lane, fine * 2) < fine
        value = value * jnp.where(along_x, velocity[0] * 0.125, velocity[1] * 0.125)
        out[:, tile, :] = value[:fields] - flux[:, tile, :]


def route_kernel(
    fine, owner_hbm, velocity_hbm, own_hbm, diffusivity_hbm, stoich_hbm, flux_hbm, matrix_hbm, sides_hbm,
    held, reflux, coefs, react, matrix, table, produced, spread, state, sums, mine,
    owner, velocity, own, diffusivity, stoich, flux, sides, w_sems,
    padded, outgoing, edges, arrived, chosen, landed, a_send, a_recv, h_send, h_recv, b_send, b_recv,
):
    me, pencil = lax.axis_index("gx"), lax.axis_index("gy")
    groups, pencils = lax.axis_size("gx"), lax.axis_size("gy")
    fields = own.shape[0]
    rows = padded.shape[0]
    half = groups // 2
    pairs = (
        (own_hbm, own), (owner_hbm, owner), (velocity_hbm, velocity), (diffusivity_hbm, diffusivity),
        (stoich_hbm, stoich), (flux_hbm, flux), (matrix_hbm, matrix), (sides_hbm, sides),
    )
    fetches = [pltpu.make_async_copy(source, target, w_sems.at[i]) for i, (source, target) in enumerate(pairs)]
    for copy in fetches:
        copy.start()
    own_in, owner_in, small_in, weights = fetches[0], fetches[1], fetches[2:5], fetches[5:]
    slots = chosen.shape[1]
    has_low, has_high = pencil > 0, pencil < pencils - 1
    around = [lax.rem(me + k, groups) for k in range(groups)]

    barrier = pltpu.get_barrier_semaphore()

    def greet(group, to):
        pl.semaphore_signal(barrier, inc=1, device_id=(group, to), device_id_type=pl.DeviceIdType.MESH)

    for group in around[1:]:
        greet(group, pencil)

    @pl.when(has_low)
    def _():
        greet(me, pencil - 1)

    @pl.when(has_high)
    def _():
        greet(me, pencil + 1)

    own_in.wait()
    padded[rows - 16 :, :] = jnp.zeros((16, padded.shape[1]), jnp.float32)
    padded[:fields, :] = own[...].astype(jnp.float32)
    for piece in range(groups):
        outgoing[piece] = padded[:, LANES * piece : LANES * (piece + 1)].astype(jnp.bfloat16)
    arrived[me] = outgoing[me]
    arrived[groups] = jnp.zeros(arrived.shape[1:], jnp.bfloat16)

    owner_in.wait()
    sources = []
    for group in around:
        for o in range(slots):
            slot = group * slots + o
            source = jnp.int32(groups)
            for q in range(groups):
                source = jnp.where(owner[q] == slot, q, source)
            sources.append(source)

    for copy in small_in:
        copy.wait()
    prepare(velocity, diffusivity, stoich, coefs, react, table)
    near = groups - 1
    pl.semaphore_wait(barrier, near + (has_low.astype(jnp.int32) + has_high.astype(jnp.int32)))

    def send(src, dst, out_sem, in_sem, group, to):
        return pltpu.make_async_remote_copy(
            src_ref=src, dst_ref=dst, send_sem=out_sem, recv_sem=in_sem,
            device_id=(group, to), device_id_type=pl.DeviceIdType.MESH,
        )

    first = [
        send(outgoing.at[group], arrived.at[me], a_send.at[k], a_recv.at[me], group, pencil)
        for k, group in enumerate(around)
    ]
    to_high = send(outgoing.at[half:], edges.at[:half], h_send.at[0], h_recv.at[0], me, pencil + 1)
    to_low = send(outgoing.at[:half], edges.at[half:], h_send.at[1], h_recv.at[1], me, pencil - 1)
    for copy in first[1:]:
        copy.start()
    pl.when(has_high)(to_high.start)
    pl.when(has_low)(to_low.start)
    for group in around[1:]:
        send(outgoing.at[group], arrived.at[group], a_send.at[0], a_recv.at[group], group, pencil).wait_recv()

    for k, group in enumerate(around):
        for o in range(slots):
            chosen[group, o] = arrived[sources[k * slots + o]]
    landed[half + me] = chosen[me]

    second = [
        send(chosen.at[group], landed.at[half + me], b_send.at[0, k], b_recv.at[half + me], group, pencil)
        for k, group in enumerate(around)
    ]
    for copy in second[1:]:
        copy.start()

    relays = []
    for k, group in enumerate(around):
        piece = landed.at[half + group]
        goes_low = jnp.logical_and(has_low, group < half)
        goes_high = jnp.logical_and(has_high, group >= half)
        over, under = half + groups + group, lax.rem(group + half, groups)
        relays.append((goes_low, send(piece, landed.at[over], b_send.at[1, k], b_recv.at[over], me, pencil - 1)))
        relays.append((goes_high, send(piece, landed.at[under], b_send.at[1, k], b_recv.at[under], me, pencil + 1)))

    def arrival(piece):
        return send(chosen.at[0], landed.at[piece], b_send.at[0, 0], b_recv.at[piece], me, pencil)

    def place(index, piece, value):
        layer, part = divmod(piece, half // 2)
        span = slice(LANES * part, LANES * (part + 1))
        if index == slots:
            mine[layer, :, span] = value
        else:
            held[index, layer, :, span] = value

    blank = jnp.zeros((rows, LANES), jnp.bfloat16)
    for piece in range(groups):
        place(slots, half + piece, outgoing[piece])

    def edge_pieces(present, incoming, pieces, start):
        @pl.when(present)
        def _():
            incoming.wait_recv()
            for piece in pieces:
                place(slots, piece, edges[start + piece - pieces[0]])

        @pl.when(jnp.logical_not(present))
        def _():
            for piece in pieces:
                for index in range(slots + 1):
                    place(index, piece, blank)

    low_pieces = list(range(half))
    high_pieces = list(range(half + groups, 2 * half + groups))
    edge_pieces(has_low, to_high, low_pieces, 0)
    edge_pieces(has_high, to_low, high_pieces, half)
    for copy in weights:
        copy.wait()
    side_sums(fine, mine, matrix, coefs, react, sides, velocity, flux, reflux, produced, spread, state, sums)

    for k, group in enumerate(around):
        if k:
            arrival(half + group).wait_recv()
        for present, copy in relays[2 * k : 2 * k + 2]:
            pl.when(present)(copy.start)
    for piece in range(groups):
        for o in range(slots):
            place(o, half + piece, landed[half + piece, o])
    for present, pieces in ((has_low, low_pieces), (has_high, high_pieces)):

        @pl.when(present)
        def _(pieces=pieces):
            for piece in pieces:
                arrival(piece).wait_recv()
                for o in range(slots):
                    place(o, piece, landed[piece, o])

    for copy in first[1:] + second[1:]:
        copy.wait_send()
    pl.when(has_high)(to_high.wait_send)
    pl.when(has_low)(to_low.wait_send)

    for present, copy in relays:
        pl.when(present)(copy.wait_send)


def route_by_kernel(fine, work, params, coarse_send, flux, patch_owner, velocity, diffusivity, stoich, matrix, sides, own_slots):
    groups = lax.axis_size("gx")
    fields, cells = coarse_send.shape[1:]
    plane = fine * fine // 4
    padded_rows = round_up(fields, 16)
    held_layers = 2 * cells // plane
    piece = (padded_rows, LANES)
    vmem = pl.BlockSpec(memory_space=pltpu.VMEM)
    anywhere = pl.BlockSpec(memory_space=pltpu.HBM)
    dma = pltpu.SemaphoreType.DMA
    bf16 = jnp.bfloat16
    tables, table = prepared(fields)
    return pl.pallas_call(
        functools.partial(route_kernel, fine),
        out_shape=(
            jax.ShapeDtypeStruct((own_slots, held_layers, padded_rows, plane), bf16),
            jax.ShapeDtypeStruct(flux.shape, jnp.float32),
        )
        + tables,
        in_specs=[anywhere] * 8,
        out_specs=(vmem,) * 4,
        scratch_shapes=[pltpu.VMEM(matrix.shape, bf16)]
        + table
        + work
        + [
            pltpu.VMEM((2 * cells // plane, round_up(fields, 8), fine * fine), jnp.float32),
            pltpu.VMEM((held_layers, padded_rows, plane), bf16),
            pltpu.SMEM(patch_owner.shape, jnp.int32),
            pltpu.SMEM(velocity.shape, jnp.float32),
            pltpu.VMEM((fields, cells), bf16),
            pltpu.VMEM(diffusivity.shape, jnp.float32),
            pltpu.VMEM(stoich.shape, jnp.float32),
            pltpu.VMEM(flux.shape, jnp.float32),
            pltpu.VMEM(sides.shape, bf16),
            dma((8,)),
            pltpu.VMEM((padded_rows, cells), jnp.float32),
            pltpu.VMEM((groups,) + piece, bf16),
            pltpu.VMEM((groups,) + piece, bf16),
            pltpu.VMEM((groups + 1,) + piece, bf16),
            pltpu.VMEM((groups, own_slots) + piece, bf16),
            pltpu.VMEM((2 * groups, own_slots) + piece, bf16),
            dma((groups,)),
            dma((groups,)),
            dma((2,)),
            dma((2,)),
            dma((2, groups)),
            dma((2 * groups,)),
        ],
        compiler_params=params(collective_id=0, has_side_effects=True),
        name="route",
    )(patch_owner, velocity, coarse_send[0], diffusivity, stoich, flux, matrix, sides)


def side_kernel(fine, velocity, coarse, matrix, diffusivity, stoich, sides, flux, out, coefs, react, table, produced, spread, state, sums):
    prepare(velocity, diffusivity, stoich, coefs, react, table)
    side_sums(fine, coarse, matrix, coefs, react, sides, velocity, flux, out, produced, spread, state, sums)


def route_by_gather(coarse_send, patch_owner, own_slots, padded_rows, plane):
    pencils = lax.axis_size("gy")
    fields, cells = coarse_send.shape[1:]
    my_slots = lax.axis_index("gx") * own_slots + jnp.arange(own_slots, dtype=jnp.int32)
    chooser = (my_slots[:, None] == patch_owner[None, :]).astype(jnp.bfloat16)
    owned = jnp.einsum(
        "oq,qfc->ofc", chooser, lax.all_gather(coarse_send, "gx", axis=0, tiled=True),
        preferred_element_type=jnp.float32,
    ).astype(jnp.bfloat16)
    both = jnp.concatenate([owned, coarse_send], 0)
    forward = [(i, i + 1) for i in range(pencils - 1)]
    backward = [(i + 1, i) for i in range(pencils - 1)]
    below = lax.ppermute(both[:, :, -2 * plane:], "gy", forward)
    above = lax.ppermute(both[:, :, : 2 * plane], "gy", backward)
    held = jnp.concatenate([below, both, above], 2)
    held = jnp.pad(held, ((0, 0), (0, padded_rows - fields), (0, 0)))
    return held.reshape(-1, padded_rows, cells // plane + 4, plane).transpose(0, 2, 1, 3)


def shards(coarse_send, coarse_flux, patch_owner, velocity, diffusivity, stoich):
    send_slots, fields, layer_cells = coarse_send.shape
    pencils = lax.axis_size("gy")
    edge = round((layer_cells * pencils) ** (1.0 / 3.0))
    fine, plane = 2 * edge, edge * edge
    layers = layer_cells // plane
    own_slots = 2 * send_slots
    rows, padded_rows = round_up(fields, 8), round_up(fields, 16)
    width = fine * fine
    deep = 2 * layers

    matrix = jnp.asarray(refine_matrix(edge), jnp.bfloat16)
    sides = jnp.asarray(side_matrix(edge), jnp.bfloat16)
    diffusivity = diffusivity.reshape(1, fields)
    fluxes = coarse_flux.reshape(send_slots, fields, -1, LANES)
    vmem = pl.BlockSpec(memory_space=pltpu.VMEM)
    smem = pl.BlockSpec(memory_space=pltpu.SMEM)
    work = [
        pltpu.VMEM((rows, width), jnp.float32),
        pltpu.VMEM(((layers + 4) * padded_rows, 2 * width), jnp.float32),
        pltpu.VMEM((deep + 4, rows, width), jnp.float32),
    ]
    params = functools.partial(pltpu.CompilerParams, vmem_limit_bytes=63 * 1024 * 1024)

    fits = send_slots == 1 and lax.axis_size("gx") * LANES == layer_cells and layers == 4 and plane == 2 * LANES
    if fits:
        held, reflux, coefs, react = route_by_kernel(
            fine, work, params, coarse_send, fluxes[0], patch_owner, velocity, diffusivity, stoich, matrix, sides, own_slots
        )
        reflux = reflux[None]
    else:
        held = route_by_gather(coarse_send, patch_owner, own_slots, padded_rows, plane)
        tables, table = prepared(fields)
        reflux = []
        for i in range(send_slots):
            one, coefs, react = pl.pallas_call(
                functools.partial(side_kernel, fine),
                out_shape=(jax.ShapeDtypeStruct(fluxes.shape[1:], jnp.float32),) + tables,
                in_specs=[smem] + [vmem] * 6,
                out_specs=(vmem,) * 3,
                scratch_shapes=table + work + [pltpu.VMEM((deep, rows, width), jnp.float32)],
                compiler_params=params(),
                name="sides",
            )(velocity, held[own_slots + i], matrix, diffusivity, stoich, sides, fluxes[i])
            reflux.append(one)
        reflux = jnp.stack(reflux)
        held = held[:own_slots]
    state = pl.pallas_call(
        functools.partial(fine_kernel, fine),
        out_shape=jax.ShapeDtypeStruct((fields, deep, own_slots * width // LANES, LANES), jnp.float32),
        in_specs=[pl.BlockSpec(memory_space=pltpu.HBM)] * 4,
        out_specs=pl.BlockSpec(memory_space=pl.ANY),
        scratch_shapes=[pltpu.VMEM(x.shape, x.dtype) for x in (held, matrix, coefs, react)]
        + [pltpu.SemaphoreType.DMA((4,))]
        + work
        + [
            pltpu.VMEM((deep + 2, rows, width), jnp.float32),
            pltpu.VMEM((deep, fields, own_slots * width // LANES, LANES), jnp.float32),
            pltpu.SemaphoreType.DMA((deep,)),
        ],
        compiler_params=params(),
        name="fine",
    )(held, matrix, coefs, react)
    state = state.reshape(fields, deep * width // LANES, own_slots, LANES).transpose(2, 0, 1, 3)
    return state.reshape(own_slots, fields, deep * width), reflux.reshape(send_slots, fields, -1)


def solution(mesh):
    placed = (P("gx", None, "gy"), P("gx", None, "gy"), P(), P(), P(), P())
    return jax.shard_map(
        shards,
        mesh=mesh,
        in_specs=placed,
        out_specs=(P("gx", None, "gy"), P("gx", None, "gy")),
        check_vma=False,
    )
```

profile of v0, /device:TPU:9, one launch (start us, length us, event | category | flops | bytes accessed | tf_op | source)
XLA Modules:
  0.0 33.2 jit_solution(2195764308053295528)
XLA Ops:
  0.6 18.1 %route.1 = (bf16[2,8,48,256]{3,2,1,0:T(8,128)(2,1)}, f32[35,2,128]{2,1,0:T(2,128)}, f32[7,40,128]{2,1,0:T(8,128)}, bf16[40,144]{1,0:T(8,128)(2,1)}) custom-call(s32[8]{0:T(128)} %owner_hbm.1, f32[3]{0:T(128)} %velocity_hbm.1, bf16[35,1024]{1,0:T(8,128)(2,1)} %bitcast.10, f32[1,35]{1,0:T(1,128)} %bitcast.13, f32[35,35]{1,0:T(8,128)} %stoich_hbm.1, ...), custom_call_target="tpu_custom_call" | custom-call | tf_op jit(solution)/shard_map/route/pallas_call | solution.py:457
  18.7 0.0 copy-start
  18.7 13.9 %fine.1 = f32[35,8,16,128]{3,2,1,0:T(8,128)} custom-call(bf16[2,8,48,256]{3,2,1,0:T(8,128)(2,1)} %get-tuple-element.6.coarse_hbm, bf16[256,2048]{1,0:T(8,128)(2,1)} %constant.4.clone.matrix_hbm, f32[7,40,128]{2,1,0:T(8,128)} %get-tuple-element.7.coefs_hbm, bf16[40,144]{1,0:T(8,128)(2,1)} %get-tuple-element.8.react_hbm), custom_call_target="tpu_custom_call" | custom-call | tf_op jit(solution)/shard_map/fine/pallas_call | solution.py:569
  32.6 0.0 copy-done
  32.6 0.6 %copy.15 = f32[1,35,256]{2,0,1:T(1,128)} copy(f32[1,35,256]{2,0,1:T(1,128)S(1)} %bitcast.11) | data formatting | bytes 71680
Async XLA Ops:
  18.7 13.9 %copy-start = (f32[35,2,128]{2,1,0:T(2,128)S(1)}, f32[35,2,128]{2,1,0:T(2,128)}, u32[]{:S(2)}) copy-start(f32[35,2,128]{2,1,0:T(2,128)} %get-tuple-element.9) | copy-start | bytes 107524
where the time goes:
time: 33.4 us; the launch traced here: 33.2 us
  Pallas kernels  32 us (96%)
  between operations  0.66 us (2%)
  local copies, waits for them, and re-layouts  0.62 us (2%)
    pallas_call x1, Pallas kernels, route_by_kernel(): pl.pallas_call(functools.partial(route_kernel, fine), out_shape=(jax.Shap...  18.1 us
    pallas_call x1, Pallas kernels, shards(): pl.pallas_call(functools.partial(fine_kernel, fine), out_shape=jax.ShapeD...  13.9 us

commit v1 on v0

--- a/solution.py
+++ b/solution.py
@@ -59,6 +59,12 @@
     reacting = jnp.concatenate([reacting, jnp.zeros((field_rows - rows, width), jnp.float32)], 0)
     high, low = split_halves(reacting)
     return jnp.dot(react[...], jnp.concatenate([high, high, low], 0), preferred_element_type=jnp.float32)
+
+
+def unrolled_layers(source, start, count, coefs, react, fine, use):
+    for layer in range(count):
+        produced = react_layer(source, start + layer, react)
+        use(layer, step_layer(source, start + layer, coefs, produced, fine))
 
 
 def run_layers(source, start, count, coefs, react, produced, fine, use):
@@ -181,14 +187,10 @@
 
 
 def fine_kernel(
-    fine, coarse_hbm, matrix_hbm, coefs_hbm, react_hbm, out, coarse, matrix, coefs, react, in_sems, produced, spread, state, middle, ready, sems,
+    fine, coarse, matrix, coefs, react, reflux, out, reflux_out, spread, state, middle, ready, sems, reflux_sem,
 ):
-    pairs = ((coarse_hbm, coarse), (matrix_hbm, matrix), (coefs_hbm, coefs), (react_hbm, react))
-    fetches = [pltpu.make_async_copy(source, target, in_sems.at[i]) for i, (source, target) in enumerate(pairs)]
-    for copy in fetches:
-        copy.start()
-    for copy in fetches[:2]:
-        copy.wait()
+    reflux_copy = pltpu.make_async_copy(reflux, reflux_out, reflux_sem.at[0])
+    reflux_copy.start()
     at_bottom, at_top = pencil_ends()
     slots = out.shape[2] * LANES // state.shape[2]
     fields = out.shape[0]
@@ -204,14 +206,10 @@
 
     for slot in range(slots):
         fill_layers(coarse.at[slot], matrix, spread, state, at_bottom, at_top)
-        if slot == 0:
-            for copy in fetches[2:]:
-                copy.wait()
-
         def to_middle(layer, pieces):
             store_layer(middle, layer, pieces)
 
-        run_layers(state, 1, layers + 2, coefs, react, produced, fine, to_middle)
+        unrolled_layers(state, 1, layers + 2, coefs, react, fine, to_middle)
 
         @pl.when(at_bottom)
         def _():
@@ -233,10 +231,11 @@
             if slot == slots - 1:
                 copy_out(layer).start()
 
-        run_layers(middle, 1, layers, coefs, react, produced, fine, to_output)
+        unrolled_layers(middle, 1, layers, coefs, react, fine, to_output)
 
     for layer in range(layers):
         copy_out(layer).wait()
+    reflux_copy.wait()
 
 
 def side_sums(fine, coarse, matrix, coefs, react, sides, velocity, flux, out, produced, spread, state, sums):
@@ -457,14 +456,14 @@
     return pl.pallas_call(
         functools.partial(route_kernel, fine),
         out_shape=(
-            jax.ShapeDtypeStruct((own_slots, held_layers, padded_rows, plane), bf16),
-            jax.ShapeDtypeStruct(flux.shape, jnp.float32),
+            pltpu.VMEM((own_slots, held_layers, padded_rows, plane), bf16),
+            pltpu.VMEM(flux.shape, jnp.float32),
         )
-        + tables,
+        + tuple(pltpu.VMEM(t.shape, t.dtype) for t in tables)
+        + (pltpu.VMEM(matrix.shape, bf16),),
         in_specs=[anywhere] * 8,
-        out_specs=(vmem,) * 4,
-        scratch_shapes=[pltpu.VMEM(matrix.shape, bf16)]
-        + table
+        out_specs=(vmem,) * 5,
+        scratch_shapes=table
         + work
         + [
             pltpu.VMEM((2 * cells // plane, round_up(fields, 8), fine * fine), jnp.float32),
@@ -492,7 +491,10 @@
         ],
         compiler_params=params(collective_id=0, has_side_effects=True),
         name="route",
-    )(patch_owner, velocity, coarse_send[0], diffusivity, stoich, flux, matrix, sides)
+    )(*(
+        pltpu.with_memory_space_constraint(x, pltpu.HBM)
+        for x in (patch_owner, velocity, coarse_send[0], diffusivity, stoich, flux, matrix, sides)
+    ))
 
 
 def side_kernel(fine, velocity, coarse, matrix, diffusivity, stoich, sides, flux, out, coefs, react, table, produced, spread, state, sums):
@@ -541,11 +543,11 @@
         pltpu.VMEM(((layers + 4) * padded_rows, 2 * width), jnp.float32),
         pltpu.VMEM((deep + 4, rows, width), jnp.float32),
     ]
-    params = functools.partial(pltpu.CompilerParams, vmem_limit_bytes=63 * 1024 * 1024)
+    params = functools.partial(pltpu.CompilerParams, vmem_limit_bytes=48 * 1024 * 1024)
 
     fits = send_slots == 1 and lax.axis_size("gx") * LANES == layer_cells and layers == 4 and plane == 2 * LANES
     if fits:
-        held, reflux, coefs, react = route_by_kernel(
+        held, reflux, coefs, react, matrix = route_by_kernel(
             fine, work, params, coarse_send, fluxes[0], patch_owner, velocity, diffusivity, stoich, matrix, sides, own_slots
         )
         reflux = reflux[None]
@@ -566,22 +568,25 @@
             reflux.append(one)
         reflux = jnp.stack(reflux)
         held = held[:own_slots]
-    state = pl.pallas_call(
+    anywhere = pl.BlockSpec(memory_space=pl.ANY)
+    state, reflux = pl.pallas_call(
         functools.partial(fine_kernel, fine),
-        out_shape=jax.ShapeDtypeStruct((fields, deep, own_slots * width // LANES, LANES), jnp.float32),
-        in_specs=[pl.BlockSpec(memory_space=pltpu.HBM)] * 4,
-        out_specs=pl.BlockSpec(memory_space=pl.ANY),
-        scratch_shapes=[pltpu.VMEM(x.shape, x.dtype) for x in (held, matrix, coefs, react)]
-        + [pltpu.SemaphoreType.DMA((4,))]
-        + work
+        out_shape=(
+            jax.ShapeDtypeStruct((fields, deep, own_slots * width // LANES, LANES), jnp.float32),
+            jax.ShapeDtypeStruct(reflux.shape, jnp.float32),
+        ),
+        in_specs=[vmem] * 5,
+        out_specs=(anywhere, anywhere),
+        scratch_shapes=work[1:]
         + [
             pltpu.VMEM((deep + 2, rows, width), jnp.float32),
             pltpu.VMEM((deep, fields, own_slots * width // LANES, LANES), jnp.float32),
             pltpu.SemaphoreType.DMA((deep,)),
+            pltpu.SemaphoreType.DMA((1,)),
         ],
         compiler_params=params(),
         name="fine",
-    )(held, matrix, coefs, react)
+    )(held, matrix, coefs, react, reflux)
     state = state.reshape(fields, deep * width // LANES, own_slots, LANES).transpose(2, 0, 1, 3)
     return state.reshape(own_slots, fields, deep * width), reflux.reshape(send_slots, fields, -1)
 

time: 33.4 us -> 26.9 us (0.81)
  Pallas kernels: 32 us -> 26.1 us
  local copies, waits for them, and re-layouts: 0.62 us -> 0 us
    pallas_call x2, Pallas kernels: 32 us -> 26.1 us  [the longest x1 17.3 us: route_by_kernel(): pl.pallas_call(functools.partial(route_kernel, fine), out_shape=(pltpu.VM...]
    unnamed x3 -> x0, local copies, waits for them, and re-layouts: 0.62 us -> none
where the time goes in v1:
time: 26.9 us; the launch traced here: 26.7 us
  Pallas kernels  26.1 us (97%)
  between operations  0.64 us (2%)
    pallas_call x1, Pallas kernels, route_by_kernel(): pl.pallas_call(functools.partial(route_kernel, fine), out_shape=(pltpu.VM...  17.3 us
    pallas_call x1, Pallas kernels, shards(): pl.pallas_call(functools.partial(fine_kernel, fine), out_shape=(jax.Shape...  8.82 us

profile of v1, /device:TPU:9, one launch (start us, length us, event | category | flops | bytes accessed | tf_op | source)
XLA Modules:
  0.0 26.7 jit_solution(9998213500779094479)
XLA Ops:
  0.6 17.3 %route.1 = (bf16[2,8,48,256]{3,2,1,0:T(8,128)(2,1)S(1)}, f32[35,2,128]{2,1,0:T(2,128)S(1)}, f32[7,40,128]{2,1,0:T(8,128)S(1)}, bf16[40,144]{1,0:T(8,128)(2,1)S(1)}, bf16[256,2048]{1,0:T(8,128)(2,1)S(1)}) custom-call(s32[8]{0:T(128)} %owner_hbm.1, f32[3]{0:T(128)} %velocity_hbm.1, bf16[35,1024]{1,0:T(8,128)(2,1)} %bitcast.11, f32[1,35]{1,0:T(1,128)} %bitcast.13, ...), custom_call_target="tpu_custom_call" | custom-call | tf_op jit(solution)/shard_map/route/pallas_call | solution.py:456
  17.9 8.8 %fine.1 = (f32[35,8,16,128]{3,2,1,0:T(8,128)}, f32[1,35,2,128]{3,2,1,0:T(2,128)}) custom-call(bf16[2,8,48,256]{3,2,1,0:T(8,128)(2,1)S(1)} %get-tuple-element.9.coarse, bf16[256,2048]{1,0:T(8,128)(2,1)S(1)} %get-tuple-element.10.matrix, f32[7,40,128]{2,1,0:T(8,128)S(1)} %get-tuple-element.11.coefs, bf16[40,144]{1,0:T(8,128)(2,1)S(1)} %get-tuple-element.12.react, ...), custom_call_target="tpu_custom_call" | custom-call | tf_op jit(solution)/shard_map/fine/pallas_call | solution.py:572

commit v2 on v1

v2 whole, which is shorter than its diff:
```python
import functools

import jax
import jax.numpy as jnp
import numpy as np
from jax import lax
from jax.experimental import pallas as pl
from jax.experimental.pallas import tpu as pltpu
from jax.sharding import PartitionSpec as P

time_step = 0.25
LANES = 128


def round_up(count, step):
    return -(-count // step) * step


def lane_groups(fine):
    return LANES // fine, fine * fine // LANES


def planes_to_tiles(columns, fine):
    groups, tiles = lane_groups(fine)
    return columns.reshape(-1, groups, tiles, fine).transpose(0, 2, 1, 3)


def refine_matrix(edge):
    fine = 2 * edge
    copy_1d = np.zeros((edge, fine), np.float32)
    slope_1d = np.zeros((edge, fine), np.float32)
    for j in range(fine):
        i, sign = j // 2, (j % 2 - 0.5) * 0.5
        copy_1d[i, j] = 1.0
        low, high = max(i - 1, 0), min(i + 1, edge - 1)
        scale = sign * (0.5 if high - low == 2 else 1.0)
        slope_1d[high, j] += scale
        slope_1d[low, j] -= scale
    copies = np.einsum("ab,cd->acbd", copy_1d, copy_1d)
    planar = copies + np.einsum("ab,cd->acbd", copy_1d, slope_1d) + np.einsum("ab,cd->acbd", slope_1d, copy_1d)
    planar = planes_to_tiles(planar, fine).reshape(edge * edge, -1)
    copies = planes_to_tiles(copies, fine)[:, ::2].reshape(edge * edge, -1)
    shifts = np.concatenate([np.eye(LANES, k=-1), np.eye(LANES, k=1)], 1)
    shifts = np.tile(shifts, (edge * edge // LANES, 1)) * (np.arange(edge * edge) < 2 * LANES)[:, None]
    return np.concatenate([planar, copies * 0.125, shifts], 1)


def side_matrix(edge):
    fine = 2 * edge
    pick = np.zeros((fine, fine, 4, edge), np.float32)
    for along in range(fine):
        pick[along, 0, 0, along // 2] = 1.0
        pick[along, fine - 1, 1, along // 2] = 1.0
        pick[0, along, 2, along // 2] = 1.0
        pick[fine - 1, along, 3, along // 2] = 1.0
    pick = planes_to_tiles(pick.reshape(fine * fine, 4 * edge).T, fine).reshape(4 * edge, -1).T
    return np.tile(pick, (1, max(1, LANES // (4 * edge))))


def split_halves(values):
    high = values.astype(jnp.bfloat16)
    low = (values - high.astype(jnp.float32)).astype(jnp.bfloat16)
    return high, low


def react_layer(source, index, react, shifts):
    rows, width = source.shape[1:]
    field_rows = react.shape[1] // 3
    cells = source[index]
    rate = 1.0 + jnp.tanh(source[index, 0:1, :])
    high, low = split_halves(jnp.concatenate([cells, jnp.zeros((field_rows - rows, width), jnp.float32)], 0))
    made = rate * jnp.dot(react[...], jnp.concatenate([high, high, low], 0), preferred_element_type=jnp.float32)
    beside = None
    if shifts is not None:
        spans = [slice(LANES * t, LANES * (t + 1)) for t in range(width // LANES)]
        joined = jnp.concatenate([jnp.concatenate([high[:, x], low[:, x]], 1) for x in spans], 0)
        beside = jnp.dot(joined, shifts, preferred_element_type=jnp.float32)
        beside = [beside[field_rows * t : field_rows * t + rows] for t in range(len(spans))]
    return made, beside


def run_layers(source, start, count, coefs, react, fine, use, together, shifts=None, layerwise=False):
    rows = source.shape[1]

    def some(first):
        layers = [first * together + i for i in range(together)]
        groups = range(rows // 8)
        produced = None if layerwise else [react_layer(source, start + layer, react, shifts) for layer in layers]
        order = [(i, g) for i in range(together) for g in groups] if layerwise else [(i, g) for g in groups for i in range(together)]
        for i, group in order:
            band = slice(8 * group, 8 * group + 8)
            held = [coefs[i, band, :] for i in range(coefs.shape[0])]
            if layerwise and group == 0:
                made, beside = react_layer(source, start + layers[i], react, shifts)
            elif not layerwise:
                made, beside = produced[i]
            use(layers[i], group, step_group(source, start + layers[i], band, held, made, beside, fine))

    if count == together:
        some(0)
    else:
        pl.loop(0, count // together)(some)


def step_group(source, index, band, coefs, produced, beside, fine):
    tiles = source.shape[2] // LANES
    cells = [source[index, band, LANES * t : LANES * (t + 1)] for t in range(tiles)]
    across = []
    for t in range(tiles):
        span = slice(LANES * t, LANES * (t + 1))
        c = cells[t]
        first, last = t == 0, t == tiles - 1
        if beside is None:
            x_high, x_low = pltpu.roll(c, LANES - 1, 1), pltpu.roll(c, 1, 1)
        else:
            x_high, x_low = beside[t][band, :LANES], beside[t][band, LANES:]
        y_high = pltpu.roll(cells[0], LANES - fine, 1) if last else cells[t + 1]
        y_low = pltpu.roll(cells[-1], fine, 1) if first else cells[t - 1]
        total = coefs[0] * x_high + coefs[1] * x_low
        total += coefs[9 if last else 2] * y_high + coefs[10 if first else 3] * y_low
        total += coefs[4] * source[index + 1, band, span] + coefs[5] * source[index - 1, band, span]
        total += coefs[7 if first else 8 if last else 6] * c
        across.append(total + produced[band, span])
    return across


def to_planes(across, fine):
    groups, tiles = lane_groups(fine)
    group = lax.broadcasted_iota(jnp.int32, (8, LANES), 1) // fine
    masks = [lax.rem(group // step, 2) == 0 for step in (1, 2)]
    out = [None] * tiles
    for first in range(0, tiles, groups):
        turned = [pltpu.roll(c, j * fine, 1) if j else c for j, c in enumerate(across[first : first + groups])]
        for a in range(groups):
            order = [turned[(g - a) % groups] for g in range(groups)]
            mixed = order[0]
            if groups == 4:
                mixed = jnp.where(masks[1], jnp.where(masks[0], *order[:2]), jnp.where(masks[0], *order[2:]))
            else:
                for g in range(1, groups):
                    mixed = jnp.where(group == g, order[g], mixed)
            out[a * (tiles // groups) + first // groups] = pltpu.roll(mixed, LANES - a * fine, 1) if a else mixed
    return out


def store_group(target, index, group, across):
    for t, value in enumerate(across):
        target[index, 8 * group : 8 * group + 8, LANES * t : LANES * (t + 1)] = value


def fill_layers(coarse, matrix, state, at_bottom, at_top):
    held, padded_rows, cells = coarse.shape
    rows, width = state.shape[1:]
    flat = coarse[...].reshape(held * padded_rows, cells)
    inner = flat[padded_rows:-padded_rows]
    chunk = 2 * LANES
    for part in range(width // 2 // chunk):
        spread = jnp.dot(flat, matrix[:, width + part * chunk : width + (part + 1) * chunk], preferred_element_type=jnp.float32)
        copies = [spread[i * padded_rows : i * padded_rows + rows] for i in range(held)]
        copies[1] = jnp.where(at_bottom, 2.0 * copies[2] - copies[3], copies[1])
        copies[-2] = jnp.where(at_top, 2.0 * copies[-3] - copies[-4], copies[-2])
        slopes = [copies[i + 1] - copies[i - 1] for i in range(1, held - 1)]
        for t in range(2):
            start = part * 2 * chunk + t * chunk
            planar = jnp.dot(inner, matrix[:, start : start + chunk], preferred_element_type=jnp.float32)
            slope = [jnp.concatenate([s[:, t * LANES : (t + 1) * LANES]] * 2, 1) for s in slopes]
            layers = []
            for i in range(held - 2):
                middle = planar[i * padded_rows : i * padded_rows + rows]
                layers += [middle - slope[i], middle + slope[i]]
            layers[1] = jnp.where(at_bottom, layers[2], layers[1])
            layers[-2] = jnp.where(at_top, layers[-3], layers[-2])
            for i, layer in enumerate(layers):
                state[i, :, start : start + chunk] = layer


def pencil_ends():
    pencil = lax.axis_index("gy")
    return pencil == 0, pencil == lax.axis_size("gy") - 1


def prepare(velocity, diffusivity, stoich, coefs, react, table, fine):
    fields = stoich.shape[0]
    rows = coefs.shape[1]
    part = react.shape[1] // 3
    table[...] = jnp.zeros(table.shape, jnp.float32)
    table[:fields, :fields] = stoich[...] * (time_step * 0.5)
    scaled = table[...]
    high = scaled.astype(jnp.bfloat16).astype(jnp.float32)
    low = scaled - high
    joined = high + pltpu.roll(low, part, 1) + pltpu.roll(high, 2 * part, 1)
    react[...] = joined[:, : 3 * part].astype(jnp.bfloat16)
    table[...] = jnp.zeros(table.shape, jnp.float32)
    table[0:1, :fields] = diffusivity[...]
    shape = (rows, LANES)
    lane = lax.broadcasted_iota(jnp.int32, shape, 1)
    diagonal = lax.broadcasted_iota(jnp.int32, shape, 0) == lane
    line = jnp.broadcast_to(table[0:1, :LANES], shape)
    column = jnp.sum(jnp.where(diagonal, line, 0.0), 1, keepdims=True)
    diffuse = jnp.broadcast_to(column, shape)
    highs = [(diffuse - velocity[dim] * 0.5) * time_step for dim in range(3)]
    lows = [(diffuse + velocity[dim] * 0.5) * time_step for dim in range(3)]
    x = lax.rem(lane, fine)
    first_x, last_x = x == 0, x == fine - 1
    first_y, last_y = lane < fine, lane >= LANES - fine
    zero = jnp.zeros(shape, jnp.float32)
    center = 1.0 - 6.0 * time_step * diffuse
    center += jnp.where(last_x, highs[0], zero) + jnp.where(first_x, lows[0], zero)
    values = [
        jnp.where(last_x, zero, highs[0]), jnp.where(first_x, zero, lows[0]), highs[1], lows[1], highs[2], lows[2],
        center, center + jnp.where(first_y, lows[1], zero), center + jnp.where(last_y, highs[1], zero),
        jnp.where(last_y, zero, highs[1]), jnp.where(first_y, zero, lows[1]),
    ]
    for i, value in enumerate(values):
        coefs[i] = value


def prepared(fields):
    rows, padded_rows = round_up(fields, 8), round_up(fields, 16)
    return (
        jax.ShapeDtypeStruct((11, rows, LANES), jnp.float32),
        jax.ShapeDtypeStruct((rows, 3 * padded_rows), jnp.bfloat16),
    ), [pltpu.VMEM((rows, round_up(3 * padded_rows, LANES)), jnp.float32)]


def fine_kernel(fine, coarse, matrix, coefs, react, reflux, out, reflux_out, state, middle, ready, sems, reflux_sem):
    reflux_copy = pltpu.make_async_copy(reflux, reflux_out, reflux_sem.at[0])
    reflux_copy.start()
    at_bottom, at_top = pencil_ends()
    slots = out.shape[2] * LANES // state.shape[2]
    shifts = matrix[:, -2 * LANES :]
    fields = out.shape[0]
    layers = out.shape[1]
    step = out.shape[2]

    def copy_out(layer, group):
        some = pl.ds(8 * group, min(8, fields - 8 * group))
        return pltpu.make_async_copy(ready.at[layer, some], out.at[some, layer], sems.at[layer, group])

    for slot in range(slots):
        fill_layers(coarse.at[slot], matrix, state, at_bottom, at_top)

        def to_middle(layer, group, across):
            store_group(middle, layer, group, across)

        run_layers(state, 1, layers + 2, coefs, react, fine, to_middle, (layers + 2) // 2)

        @pl.when(at_bottom)
        def _():
            middle[0] = middle[1]

        @pl.when(at_top)
        def _():
            middle[layers + 1] = middle[layers]

        def to_output(layer, group, across):
            low, high = 8 * group, min(8 * group + 8, fields)
            halves = []
            for t, value in enumerate(across):
                span = slice(LANES * t, LANES * (t + 1))
                halves.append((value + state[layer + 2, low : low + 8, span]) * 0.5)
            lines = ready.at[layer].reshape(fields * step, LANES)
            for t, value in enumerate(to_planes(halves, fine)):
                lines[pl.ds(low * step + t * slots + slot, high - low, stride=step), :] = value[: high - low]
            if slot == slots - 1:
                copy_out(layer, group).start()

        run_layers(middle, 1, layers, coefs, react, fine, to_output, layers, shifts, True)

    for layer in range(layers):
        for group in range(sems.shape[1]):
            copy_out(layer, group).wait()
    reflux_copy.wait()


def side_sums(fine, coarse, matrix, coefs, react, sides, velocity, flux, out, state, sums):
    at_bottom, at_top = pencil_ends()
    fields = out.shape[0]
    rows, width = state.shape[1:]
    layers = state.shape[0] - 4
    fill_layers(coarse, matrix, state, at_bottom, at_top)

    def to_sums(layer, group, across):
        band = slice(8 * group, 8 * group + 8)
        for t, value in enumerate(across):
            span = slice(LANES * t, LANES * (t + 1))
            sums[layer, band, span] = value + state[layer + 2, band, span]

    run_layers(state, 2, layers, coefs, react, fine, to_sums, 2)
    pads = jnp.zeros((round_up(rows, 16) - rows, width), jnp.float32)
    halves = []
    for pair in range(layers // 2):
        high, low = split_halves(jnp.concatenate([sums[2 * pair] + sums[2 * pair + 1], pads], 0))
        halves += [high, low]
    picked = jnp.dot(jnp.concatenate(halves, 0), sides[...], preferred_element_type=jnp.float32)
    step = rows + pads.shape[0]
    each = [
        picked[2 * step * i : 2 * step * i + rows] + picked[2 * step * i + step : 2 * step * i + step + rows]
        for i in range(layers // 2)
    ]
    span = sides.shape[1]
    per_tile = span // (fine * 2)
    lane = lax.broadcasted_iota(jnp.int32, (rows, span), 1)
    for tile in range(len(each) // per_tile):
        value = each[tile * per_tile]
        for i in range(1, per_tile):
            value = jnp.where(lane >= i * fine * 2, each[tile * per_tile + i], value)
        along_x = lax.rem(lane, fine * 2) < fine
        value = value * jnp.where(along_x, velocity[0] * 0.125, velocity[1] * 0.125)
        out[:, tile, :] = value[:fields] - flux[:, tile, :]


def route_kernel(
    fine, owner_hbm, velocity_hbm, own_hbm, diffusivity_hbm, stoich_hbm, flux_hbm, matrix_hbm, sides_hbm,
    held, reflux, coefs, react, matrix, table, state, sums, mine,
    owner, velocity, own, diffusivity, stoich, flux, sides, w_sems,
    outgoing, edges, arrived, chosen, landed, a_send, a_recv, h_send, h_recv, b_send, b_recv,
):
    me, pencil = lax.axis_index("gx"), lax.axis_index("gy")
    groups, pencils = lax.axis_size("gx"), lax.axis_size("gy")
    fields = own.shape[0]
    rows, sent = outgoing.shape[1], round_up(fields, 8)
    half = groups // 2
    pairs = (
        (own_hbm, own), (owner_hbm, owner), (velocity_hbm, velocity), (diffusivity_hbm, diffusivity),
        (stoich_hbm, stoich), (flux_hbm, flux), (matrix_hbm, matrix), (sides_hbm, sides),
    )
    fetches = [pltpu.make_async_copy(source, target, w_sems.at[i]) for i, (source, target) in enumerate(pairs)]
    for copy in fetches:
        copy.start()
    own_in, owner_in, small_in, weights = fetches[0], fetches[1], fetches[2:5], fetches[5:]
    slots = chosen.shape[1]
    has_low, has_high = pencil > 0, pencil < pencils - 1
    around = [lax.rem(me + k, groups) for k in range(groups)]

    barrier = pltpu.get_barrier_semaphore()

    def greet(group, to):
        pl.semaphore_signal(barrier, inc=1, device_id=(group, to), device_id_type=pl.DeviceIdType.MESH)

    for group in around[1:]:
        greet(group, pencil)

    @pl.when(has_low)
    def _():
        greet(me, pencil - 1)

    @pl.when(has_high)
    def _():
        greet(me, pencil + 1)

    own_in.wait()
    for piece in range(groups):
        outgoing[piece, :fields] = own[:, LANES * piece : LANES * (piece + 1)]
        outgoing[piece, fields:] = jnp.zeros((rows - fields, LANES), jnp.bfloat16)
    arrived[me] = outgoing[me]
    arrived[groups] = jnp.zeros(arrived.shape[1:], jnp.bfloat16)

    near = groups - 1
    pl.semaphore_wait(barrier, near + (has_low.astype(jnp.int32) + has_high.astype(jnp.int32)))

    def send(src, dst, out_sem, in_sem, group, to):
        return pltpu.make_async_remote_copy(
            src_ref=src, dst_ref=dst, send_sem=out_sem, recv_sem=in_sem,
            device_id=(group, to), device_id_type=pl.DeviceIdType.MESH,
        )

    first = [
        send(outgoing.at[group, :sent], arrived.at[me, :sent], a_send.at[k], a_recv.at[me], group, pencil)
        for k, group in enumerate(around)
    ]
    to_high = send(outgoing.at[half:, :sent], edges.at[:half, :sent], h_send.at[0], h_recv.at[0], me, pencil + 1)
    to_low = send(outgoing.at[:half, :sent], edges.at[half:, :sent], h_send.at[1], h_recv.at[1], me, pencil - 1)
    for copy in first[1:]:
        copy.start()
    pl.when(has_high)(to_high.start)
    pl.when(has_low)(to_low.start)
    owner_in.wait()
    sources = []
    for group in around:
        for o in range(slots):
            slot = group * slots + o
            source = jnp.int32(groups)
            for q in range(groups):
                source = jnp.where(owner[q] == slot, q, source)
            sources.append(source)

    for copy in small_in:
        copy.wait()
    prepare(velocity, diffusivity, stoich, coefs, react, table, fine)
    for group in around[1:]:
        send(outgoing.at[group, :sent], arrived.at[group, :sent], a_send.at[0], a_recv.at[group], group, pencil).wait_recv()

    for k, group in enumerate(around):
        for o in range(slots):
            chosen[group, o, :sent] = arrived[sources[k * slots + o], :sent]
    landed[half + me, :, :sent] = chosen[me, :, :sent]

    second = [
        send(chosen.at[group, :, :sent], landed.at[half + me, :, :sent], b_send.at[0, k], b_recv.at[half + me], group, pencil)
        for k, group in enumerate(around)
    ]
    for copy in second[1:]:
        copy.start()

    relays = []
    for k, group in enumerate(around):
        piece = landed.at[half + group, :, :sent]
        goes_low = jnp.logical_and(has_low, group < half)
        goes_high = jnp.logical_and(has_high, group >= half)
        over, under = half + groups + group, lax.rem(group + half, groups)
        relays.append((goes_low, send(piece, landed.at[over, :, :sent], b_send.at[1, k], b_recv.at[over], me, pencil - 1)))
        relays.append((goes_high, send(piece, landed.at[under, :, :sent], b_send.at[1, k], b_recv.at[under], me, pencil + 1)))

    def arrival(piece):
        return send(chosen.at[0, :, :sent], landed.at[piece, :, :sent], b_send.at[0, 0], b_recv.at[piece], me, pencil)

    def place(index, piece, value):
        layer, part = divmod(piece, half // 2)
        span = slice(LANES * part, LANES * (part + 1))
        if index == slots:
            mine[layer, : value.shape[0], span] = value
        else:
            held[index, layer, : value.shape[0], span] = value

    blank = jnp.zeros((rows, LANES), jnp.bfloat16)
    for layer in range(mine.shape[0]):
        for index in range(slots):
            held[index, layer, sent:, :] = jnp.zeros((rows - sent, held.shape[3]), jnp.bfloat16)
        mine[layer, sent:, :] = jnp.zeros((rows - sent, held.shape[3]), jnp.bfloat16)
    for piece in range(groups):
        place(slots, half + piece, outgoing[piece])

    def edge_pieces(present, incoming, pieces, start):
        @pl.when(present)
        def _():
            incoming.wait_recv()
            for piece in pieces:
                place(slots, piece, edges[start + piece - pieces[0], :sent])

        @pl.when(jnp.logical_not(present))
        def _():
            for piece in pieces:
                for index in range(slots + 1):
                    place(index, piece, blank)

    low_pieces = list(range(half))
    high_pieces = list(range(half + groups, 2 * half + groups))
    edge_pieces(has_low, to_high, low_pieces, 0)
    edge_pieces(has_high, to_low, high_pieces, half)
    for copy in weights:
        copy.wait()
    side_sums(fine, mine, matrix, coefs, react, sides, velocity, flux, reflux, state, sums)

    for k, group in enumerate(around):
        if k:
            arrival(half + group).wait_recv()
        for present, copy in relays[2 * k : 2 * k + 2]:
            pl.when(present)(copy.start)
    for piece in range(groups):
        for o in range(slots):
            place(o, half + piece, landed[half + piece, o, :sent])
    for present, pieces in ((has_low, low_pieces), (has_high, high_pieces)):

        @pl.when(present)
        def _(pieces=pieces):
            for piece in pieces:
                arrival(piece).wait_recv()
                for o in range(slots):
                    place(o, piece, landed[piece, o, :sent])

    for copy in first[1:] + second[1:]:
        copy.wait_send()
    pl.when(has_high)(to_high.wait_send)
    pl.when(has_low)(to_low.wait_send)

    for present, copy in relays:
        pl.when(present)(copy.wait_send)


def route_by_kernel(fine, work, params, coarse_send, flux, patch_owner, velocity, diffusivity, stoich, matrix, sides, own_slots):
    groups = lax.axis_size("gx")
    fields, cells = coarse_send.shape[1:]
    plane = fine * fine // 4
    padded_rows = round_up(fields, 16)
    held_layers = 2 * cells // plane
    piece = (padded_rows, LANES)
    vmem = pl.BlockSpec(memory_space=pltpu.VMEM)
    anywhere = pl.BlockSpec(memory_space=pltpu.HBM)
    dma = pltpu.SemaphoreType.DMA
    bf16 = jnp.bfloat16
    tables, table = prepared(fields)
    return pl.pallas_call(
        functools.partial(route_kernel, fine),
        out_shape=(
            pltpu.VMEM((own_slots, held_layers, padded_rows, plane), bf16),
            pltpu.VMEM(flux.shape, jnp.float32),
        )
        + tuple(pltpu.VMEM(t.shape, t.dtype) for t in tables)
        + (pltpu.VMEM(matrix.shape, bf16),),
        in_specs=[anywhere] * 8,
        out_specs=(vmem,) * 5,
        scratch_shapes=table
        + work
        + [
            pltpu.VMEM((2 * cells // plane, round_up(fields, 8), fine * fine), jnp.float32),
            pltpu.VMEM((held_layers, padded_rows, plane), bf16),
            pltpu.SMEM(patch_owner.shape, jnp.int32),
            pltpu.SMEM(velocity.shape, jnp.float32),
            pltpu.VMEM((fields, cells), bf16),
            pltpu.VMEM(diffusivity.shape, jnp.float32),
            pltpu.VMEM(stoich.shape, jnp.float32),
            pltpu.VMEM(flux.shape, jnp.float32),
            pltpu.VMEM(sides.shape, bf16),
            dma((8,)),
            pltpu.VMEM((groups,) + piece, bf16),
            pltpu.VMEM((groups,) + piece, bf16),
            pltpu.VMEM((groups + 1,) + piece, bf16),
            pltpu.VMEM((groups, own_slots) + piece, bf16),
            pltpu.VMEM((2 * groups, own_slots) + piece, bf16),
            dma((groups,)),
            dma((groups,)),
            dma((2,)),
            dma((2,)),
            dma((2, groups)),
            dma((2 * groups,)),
        ],
        compiler_params=params(collective_id=0, has_side_effects=True),
        name="route",
    )(*(
        pltpu.with_memory_space_constraint(x, pltpu.HBM)
        for x in (patch_owner, velocity, coarse_send[0], diffusivity, stoich, flux, matrix, sides)
    ))


def side_kernel(fine, velocity, coarse, matrix, diffusivity, stoich, sides, flux, out, coefs, react, table, state, sums):
    prepare(velocity, diffusivity, stoich, coefs, react, table, fine)
    side_sums(fine, coarse, matrix, coefs, react, sides, velocity, flux, out, state, sums)


def route_by_gather(coarse_send, patch_owner, own_slots, padded_rows, plane):
    pencils = lax.axis_size("gy")
    fields, cells = coarse_send.shape[1:]
    my_slots = lax.axis_index("gx") * own_slots + jnp.arange(own_slots, dtype=jnp.int32)
    chooser = (my_slots[:, None] == patch_owner[None, :]).astype(jnp.bfloat16)
    owned = jnp.einsum(
        "oq,qfc->ofc", chooser, lax.all_gather(coarse_send, "gx", axis=0, tiled=True),
        preferred_element_type=jnp.float32,
    ).astype(jnp.bfloat16)
    both = jnp.concatenate([owned, coarse_send], 0)
    forward = [(i, i + 1) for i in range(pencils - 1)]
    backward = [(i + 1, i) for i in range(pencils - 1)]
    below = lax.ppermute(both[:, :, -2 * plane:], "gy", forward)
    above = lax.ppermute(both[:, :, : 2 * plane], "gy", backward)
    held = jnp.concatenate([below, both, above], 2)
    held = jnp.pad(held, ((0, 0), (0, padded_rows - fields), (0, 0)))
    return held.reshape(-1, padded_rows, cells // plane + 4, plane).transpose(0, 2, 1, 3)


def shards(coarse_send, coarse_flux, patch_owner, velocity, diffusivity, stoich):
    send_slots, fields, layer_cells = coarse_send.shape
    pencils = lax.axis_size("gy")
    edge = round((layer_cells * pencils) ** (1.0 / 3.0))
    fine, plane = 2 * edge, edge * edge
    layers = layer_cells // plane
    own_slots = 2 * send_slots
    rows, padded_rows = round_up(fields, 8), round_up(fields, 16)
    width = fine * fine
    deep = 2 * layers

    matrix = jnp.asarray(refine_matrix(edge), jnp.bfloat16)
    sides = jnp.asarray(side_matrix(edge), jnp.bfloat16)
    diffusivity = diffusivity.reshape(1, fields)
    fluxes = coarse_flux.reshape(send_slots, fields, -1, LANES)
    vmem = pl.BlockSpec(memory_space=pltpu.VMEM)
    smem = pl.BlockSpec(memory_space=pltpu.SMEM)
    work = [pltpu.VMEM((deep + 4, rows, width), jnp.float32)]
    params = functools.partial(pltpu.CompilerParams, vmem_limit_bytes=48 * 1024 * 1024)

    fits = send_slots == 1 and lax.axis_size("gx") * LANES == layer_cells and layers == 4 and plane == 2 * LANES
    if fits:
        held, reflux, coefs, react, matrix = route_by_kernel(
            fine, work, params, coarse_send, fluxes[0], patch_owner, velocity, diffusivity, stoich, matrix, sides, own_slots
        )
        reflux = reflux[None]
    else:
        held = route_by_gather(coarse_send, patch_owner, own_slots, padded_rows, plane)
        tables, table = prepared(fields)
        reflux = []
        for i in range(send_slots):
            one, coefs, react = pl.pallas_call(
                functools.partial(side_kernel, fine),
                out_shape=(jax.ShapeDtypeStruct(fluxes.shape[1:], jnp.float32),) + tables,
                in_specs=[smem] + [vmem] * 6,
                out_specs=(vmem,) * 3,
                scratch_shapes=table + work + [pltpu.VMEM((deep, rows, width), jnp.float32)],
                compiler_params=params(),
                name="sides",
            )(velocity, held[own_slots + i], matrix, diffusivity, stoich, sides, fluxes[i])
            reflux.append(one)
        reflux = jnp.stack(reflux)
        held = held[:own_slots]
    anywhere = pl.BlockSpec(memory_space=pl.ANY)
    state, reflux = pl.pallas_call(
        functools.partial(fine_kernel, fine),
        out_shape=(
            jax.ShapeDtypeStruct((fields, deep, own_slots * width // LANES, LANES), jnp.float32),
            jax.ShapeDtypeStruct(reflux.shape, jnp.float32),
        ),
        in_specs=[vmem] * 5,
        out_specs=(anywhere, anywhere),
        scratch_shapes=work
        + [
            pltpu.VMEM((deep + 2, rows, width), jnp.float32),
            pltpu.VMEM((deep, fields, own_slots * width // LANES, LANES), jnp.float32),
            pltpu.SemaphoreType.DMA((deep, rows // 8)),
            pltpu.SemaphoreType.DMA((1,)),
        ],
        compiler_params=params(),
        name="fine",
    )(held, matrix, coefs, react, reflux)
    state = state.reshape(fields, deep * width // LANES, own_slots, LANES).transpose(2, 0, 1, 3)
    return state.reshape(own_slots, fields, deep * width), reflux.reshape(send_slots, fields, -1)


def solution(mesh):
    placed = (P("gx", None, "gy"), P("gx", None, "gy"), P(), P(), P(), P())
    return jax.shard_map(
        shards,
        mesh=mesh,
        in_specs=placed,
        out_specs=(P("gx", None, "gy"), P("gx", None, "gy")),
        check_vma=False,
    )
```

time: 26.9 us -> 25.8 us (0.959)
  Pallas kernels: 26.1 us -> 25 us
    pallas_call x1, Pallas kernels: 8.82 us -> 8.2 us  [shards(): pl.pallas_call(functools.partial(fine_kernel, fine), out_shape=(jax.Shape...]
    pallas_call x1, Pallas kernels: 17.3 us -> 16.8 us  [route_by_kernel(): pl.pallas_call(functools.partial(route_kernel, fine), out_shape=(pltpu.VM...]
where the time goes in v2:
time: 25.8 us; the launch traced here: 25.6 us
  Pallas kernels  25 us (97%)
  between operations  0.64 us (2%)
    pallas_call x1, Pallas kernels, route_by_kernel(): pl.pallas_call(functools.partial(route_kernel, fine), out_shape=(pltpu.VM...  16.8 us
    pallas_call x1, Pallas kernels, shards(): pl.pallas_call(functools.partial(fine_kernel, fine), out_shape=(jax.Shape...  8.2 us

profile of v2, /device:TPU:9, one launch (start us, length us, event | category | flops | bytes accessed | tf_op | source)
XLA Modules:
  0.0 25.6 jit_solution(4239116008203936659)
XLA Ops:
  0.6 16.8 %route.1 = (bf16[2,8,48,256]{3,2,1,0:T(8,128)(2,1)S(1)}, f32[35,2,128]{2,1,0:T(2,128)S(1)}, f32[11,40,128]{2,1,0:T(8,128)S(1)}, bf16[40,144]{1,0:T(8,128)(2,1)S(1)}, bf16[256,1792]{1,0:T(8,128)(2,1)S(1)}) custom-call(s32[8]{0:T(128)} %owner_hbm.1, f32[3]{0:T(128)} %velocity_hbm.1, bf16[35,1024]{1,0:T(8,128)(2,1)} %bitcast.11, f32[1,35]{1,0:T(1,128)} %bitcast.13, ...), custom_call_target="tpu_custom_call" | custom-call | tf_op jit(solution)/shard_map/route/pallas_call | solution.py:493
  17.4 8.2 %fine.1 = (f32[35,8,16,128]{3,2,1,0:T(8,128)}, f32[1,35,2,128]{3,2,1,0:T(2,128)}) custom-call(bf16[2,8,48,256]{3,2,1,0:T(8,128)(2,1)S(1)} %get-tuple-element.9.coarse, bf16[256,1792]{1,0:T(8,128)(2,1)S(1)} %get-tuple-element.10.matrix, f32[11,40,128]{2,1,0:T(8,128)S(1)} %get-tuple-element.11.coefs, bf16[40,144]{1,0:T(8,128)(2,1)S(1)} %get-tuple-element.12.react, ...), custom_call_target="tpu_custom_call" | custom-call | tf_op jit(solution)/shard_map/fine/pallas_call | solution.py:604

commit v3 on v2

--- a/solution.py
+++ b/solution.py
@@ -243,7 +243,7 @@
         def to_middle(layer, group, across):
             store_group(middle, layer, group, across)
 
-        run_layers(state, 1, layers + 2, coefs, react, fine, to_middle, (layers + 2) // 2)
+        run_layers(state, 1, layers + 2, coefs, react, fine, to_middle, (layers + 2) // 2, None, True)
 
         @pl.when(at_bottom)
         def _():
@@ -319,7 +319,7 @@
     me, pencil = lax.axis_index("gx"), lax.axis_index("gy")
     groups, pencils = lax.axis_size("gx"), lax.axis_size("gy")
     fields = own.shape[0]
-    rows, sent = outgoing.shape[1], round_up(fields, 8)
+    rows, sent = outgoing.shape[1], round_up(fields, 4)
     half = groups // 2
     pairs = (
         (own_hbm, own), (owner_hbm, owner), (velocity_hbm, velocity), (diffusivity_hbm, diffusivity),
@@ -371,8 +371,8 @@
     ]
     to_high = send(outgoing.at[half:, :sent], edges.at[:half, :sent], h_send.at[0], h_recv.at[0], me, pencil + 1)
     to_low = send(outgoing.at[:half, :sent], edges.at[half:, :sent], h_send.at[1], h_recv.at[1], me, pencil - 1)
-    for copy in first[1:]:
-        copy.start()
+    for k in sorted(range(1, groups), key=lambda k: min(k, groups - k)):
+        first[k].start()
     pl.when(has_high)(to_high.start)
     pl.when(has_low)(to_low.start)
     owner_in.wait()

time: 25.8 us -> 25.1 us (0.973)
  Pallas kernels: 25 us -> 24.3 us
    pallas_call x1, Pallas kernels: 16.8 us -> 16.2 us  [route_by_kernel(): pl.pallas_call(functools.partial(route_kernel, fine), out_shape=(pltpu.VM...]
where the time goes in v3:
time: 25.1 us; the launch traced here: 25 us
  Pallas kernels  24.3 us (97%)
  between operations  0.64 us (3%)
    pallas_call x1, Pallas kernels, route_by_kernel(): pl.pallas_call(functools.partial(route_kernel, fine), out_shape=(pltpu.VM...  16.2 us
    pallas_call x1, Pallas kernels, shards(): pl.pallas_call(functools.partial(fine_kernel, fine), out_shape=(jax.Shape...  8.1 us

profile of v3, /device:TPU:9, one launch (start us, length us, event | category | flops | bytes accessed | tf_op | source)
XLA Modules:
  0.0 25.0 jit_solution(12106973870507177283)
XLA Ops:
  0.6 16.2 %route.1 = (bf16[2,8,48,256]{3,2,1,0:T(8,128)(2,1)S(1)}, f32[35,2,128]{2,1,0:T(2,128)S(1)}, f32[11,40,128]{2,1,0:T(8,128)S(1)}, bf16[40,144]{1,0:T(8,128)(2,1)S(1)}, bf16[256,1792]{1,0:T(8,128)(2,1)S(1)}) custom-call(s32[8]{0:T(128)} %owner_hbm.1, f32[3]{0:T(128)} %velocity_hbm.1, bf16[35,1024]{1,0:T(8,128)(2,1)} %bitcast.11, f32[1,35]{1,0:T(1,128)} %bitcast.13, ...), custom_call_target="tpu_custom_call" | custom-call | tf_op jit(solution)/shard_map/route/pallas_call | solution.py:493
  16.9 8.1 %fine.1 = (f32[35,8,16,128]{3,2,1,0:T(8,128)}, f32[1,35,2,128]{3,2,1,0:T(2,128)}) custom-call(bf16[2,8,48,256]{3,2,1,0:T(8,128)(2,1)S(1)} %get-tuple-element.9.coarse, bf16[256,1792]{1,0:T(8,128)(2,1)S(1)} %get-tuple-element.10.matrix, f32[11,40,128]{2,1,0:T(8,128)S(1)} %get-tuple-element.11.coefs, bf16[40,144]{1,0:T(8,128)(2,1)S(1)} %get-tuple-element.12.react, ...), custom_call_target="tpu_custom_call" | custom-call | tf_op jit(solution)/shard_map/fine/pallas_call | solution.py:604
